TPU v7x, 32 devices: a whole 2x2x4 slice. The times are simulated.
32 devices in a mesh: gx: 8 (over z, x), gy: 2 (over core), gz: 2 (over y).
Axes of the slice: x: 2, y: 2, z: 4, core: 2. Of those that a mesh axis runs over, the one named last changes fastest.
Arguments:
- positions: float32 [16, 8, 8, 8, 3], P('gx', 'gy', 'gz'), may hold values from 0 to 1
- species: int32 [16, 8, 8, 8], P('gx', 'gy', 'gz'), may hold values from 0 to 3
- neighbors: int32 [16, 8, 8, 8, 16], P('gx', 'gy', 'gz'), may hold values from 0 to 215, as said below
- edge_mask: int32 [16, 8, 8, 8, 16], P('gx', 'gy', 'gz'), may hold values 0 or 1
- species_embed: float32 [4, 128], replicated, may hold values from -6 to 6
- radial_weight: float32 [2, 8, 384], replicated, may hold values from -6 to 6
- mix_weight: float32 [2, 384, 128], replicated, may hold values from -0.3125 to 0.3125
- readout: float32 [128], replicated, may hold values from -0.5 to 0.5
- energy_offset: float32 [4], replicated, may hold values from -6 to 6
Outputs:
- atom_energy: float32 [16, 8, 8, 8], P('gx', 'gy', 'gz')
- forces: float32 [16, 8, 8, 8, 3], P('gx', 'gy', 'gz')
Inputs may be any that keep to these rules, and one draw needn't show every extreme that they name: `neighbors`: each entry lies in 0 to 215 and names slot n mod 8 of the cell at offset (n // 72 - 1, (n // 24) mod 3 - 1, (n // 8) mod 3 - 1), periodic; it never names the receiving atom itself (104 plus its own slot). Repeats may occur.
All inputs are finite; a program needn't handle non-finite values.
Results may differ from a plain program's by a relative error of at most 0.0003.
Values sent between devices are 32-bit elements.
A program may use at most 128 MiB of HBM per device.

v0:
```python
import functools
import itertools
import math

import jax
import jax.numpy as jnp
from jax import lax
from jax.experimental import pallas as pl
from jax.experimental.pallas import tpu as pltpu
from jax.sharding import PartitionSpec as P

F32 = jnp.float32
BF16 = jnp.bfloat16
MESH = pl.DeviceIdType.MESH
AXES = ("gx", "gy", "gz")
RC = 2.0
NO_EDGE = 1023
OFFSETS = [o for o in itertools.product((-1, 0, 1), repeat=3) if any(o)]
ORDERS = ((0, 1), (1, 4), (4, 9))
VM = pl.BlockSpec(memory_space=pltpu.VMEM)

NN = ((1,), (0,))
NT = ((1,), (1,))
TN = ((0,), (0,))


def split(x):
    hi = x.astype(BF16)
    return hi, (x - hi.astype(F32)).astype(BF16)


def split32(x):
    hi = x.astype(BF16).astype(F32)
    return hi, x - hi


def mm(a, b, dims):
    return lax.dot_general(a, b, (dims, ((), ())), preferred_element_type=F32)


def mm3(a, b, dims):
    return mm(a[0], b[0], dims) + (mm(a[0], b[1], dims) + mm(a[1], b[0], dims))


def peer(o):
    ids = []
    for axis, step in zip(AXES, o):
        n = lax.axis_size(axis)
        ids.append(lax.rem(lax.axis_index(axis) + (step + n), n))
    return tuple(ids)


def greet():
    barrier = pltpu.get_barrier_semaphore()
    for o in OFFSETS:
        pl.semaphore_signal(barrier, inc=1, device_id=peer(o), device_id_type=MESH)
    pl.semaphore_wait(barrier, len(OFFSETS))


def box(o, dims, minus, zero, plus):
    out = []
    for s, n in zip(o, dims):
        out.append(zero(n) if s == 0 else (plus(n) if s > 0 else minus(n)))
    return tuple(out)


def face(o, dims):
    return box(o, dims, lambda n: pl.ds(0, 1), lambda n: pl.ds(0, n), lambda n: pl.ds(n - 1, 1))


def halo(o, dims):
    return box(o, dims, lambda n: pl.ds(0, 1), lambda n: pl.ds(1, n), lambda n: pl.ds(n + 1, 1))


def opposite(o):
    return tuple(-s for s in o)


def spread_kernel(dims, own_ref, ext_ref, send_sem, recv_sem, local_sem):
    greet()
    inner = tuple(pl.ds(1, n) for n in dims)
    local = pltpu.make_async_copy(own_ref, ext_ref.at[inner], local_sem)
    local.start()
    copies = []
    for i, o in enumerate(OFFSETS):
        copies.append(
            pltpu.make_async_remote_copy(
                src_ref=own_ref.at[face(o, dims)],
                dst_ref=ext_ref.at[halo(opposite(o), dims)],
                send_sem=send_sem.at[i],
                recv_sem=recv_sem.at[i],
                device_id=peer(o),
                device_id_type=MESH,
            )
        )
        copies[-1].start()
    local.wait()
    for copy in copies:
        copy.wait()


def spread(own, cid):
    dims = own.shape[:3]
    n = len(OFFSETS)
    return pl.pallas_call(
        functools.partial(spread_kernel, dims),
        out_shape=jax.ShapeDtypeStruct(tuple(d + 2 for d in dims) + own.shape[3:], own.dtype),
        in_specs=[VM],
        out_specs=VM,
        scratch_shapes=[
            pltpu.SemaphoreType.DMA((n,)),
            pltpu.SemaphoreType.DMA((n,)),
            pltpu.SemaphoreType.DMA,
        ],
        compiler_params=pltpu.CompilerParams(collective_id=cid, has_side_effects=True),
        name=f"spread_{cid}",
    )(own)


def fold_kernel(dims, ext_ref, own_ref, recv, send_sem, recv_sem):
    greet()
    copies = []
    for i, o in enumerate(OFFSETS):
        copies.append(
            pltpu.make_async_remote_copy(
                src_ref=ext_ref.at[halo(o, dims)],
                dst_ref=recv.at[halo(o, dims)],
                send_sem=send_sem.at[i],
                recv_sem=recv_sem.at[i],
                device_id=peer(o),
                device_id_type=MESH,
            )
        )
        copies[-1].start()
    own_ref[...] = ext_ref[tuple(pl.ds(1, n) for n in dims)]
    for o, copy in zip(OFFSETS, copies):
        copy.wait()
        at = face(opposite(o), dims)
        own_ref[at] = own_ref[at] + recv[halo(o, dims)]


def fold(ext, cid):
    dims = tuple(d - 2 for d in ext.shape[:3])
    n = len(OFFSETS)
    return pl.pallas_call(
        functools.partial(fold_kernel, dims),
        out_shape=jax.ShapeDtypeStruct(dims + ext.shape[3:], ext.dtype),
        in_specs=[VM],
        out_specs=VM,
        scratch_shapes=[
            pltpu.VMEM(ext.shape, ext.dtype),
            pltpu.SemaphoreType.DMA((n,)),
            pltpu.SemaphoreType.DMA((n,)),
        ],
        compiler_params=pltpu.CompilerParams(collective_id=cid, has_side_effects=True),
        name=f"fold_{cid}",
    )(ext)


def iota(shape, dim):
    return lax.broadcasted_iota(jnp.int32, shape, dim)


def slot_mask(slots, lanes):
    per = lanes // slots
    lane, row = iota((slots, lanes), 1), iota((slots, lanes), 0)
    return jnp.where((lane >= row * per) & (lane < row * per + per), 1.0, 0.0).astype(F32)


def basis(geom, nb):
    dx, dy, dz, ms = geom[0:1], geom[1:2], geom[2:3], geom[4:5]
    r2 = dx * dx + dy * dy + dz * dz
    r = jnp.sqrt(r2)
    inside = r < RC
    w = 1.0 - r2 * (1.0 / RC**2)
    u = jnp.where(inside, w * w, 0.0)
    mu = iota((nb, geom.shape[1]), 0).astype(F32) * (RC / (nb - 1))
    g = ((nb - 1) / RC) ** 2
    off = r - mu
    gauss = jnp.exp(-g * off * off)
    rb = gauss * u
    px, py, pz = dx / RC, dy / RC, dz / RC
    c3, c5, c15 = math.sqrt(3.0), math.sqrt(5.0), math.sqrt(15.0)
    ys = [
        ms,
        ms * (c3 * px),
        ms * (c3 * py),
        ms * (c3 * pz),
        ms * (c15 * px * py),
        ms * (c15 * py * pz),
        ms * ((0.5 * c5) * (3.0 * pz * pz - (px * px + py * py + pz * pz))),
        ms * (c15 * px * pz),
        ms * ((0.5 * c15) * (px * px - py * py)),
    ]
    return rb, ys, (r, w, inside, gauss, off, g, (px, py, pz))


def geom_pull(geom, extra, d_rb, d_y):
    r, w, inside, gauss, off, g, (px, py, pz) = extra
    ms = geom[4:5]
    du = jnp.where(inside, -r * w, 0.0)
    u = jnp.where(inside, w * w, 0.0)
    d_r = jnp.sum(d_rb * gauss * (du - 2.0 * g * off * u), 0, keepdims=True)
    c3, c5, c15 = math.sqrt(3.0), math.sqrt(5.0), math.sqrt(15.0)
    gy = [ms * d_y[m : m + 1] for m in range(9)]
    vx = c3 * gy[1] + c15 * (py * gy[4] + pz * gy[7] + px * gy[8]) - c5 * px * gy[6]
    vy = c3 * gy[2] + c15 * (px * gy[4] + pz * gy[5] - py * gy[8]) - c5 * py * gy[6]
    vz = c3 * gy[3] + c15 * (py * gy[5] + px * gy[7]) + 2.0 * c5 * pz * gy[6]
    k = d_r / jnp.maximum(r, 1e-20)
    return [v / RC + k * geom[i : i + 1] for i, v in enumerate((vx, vy, vz))]


def stack3(x, order):
    hi, lo = split32(x)
    parts = {"h": hi, "l": lo}
    rows = [parts[o] for o in order]
    pad = -(3 * x.shape[0]) % 16
    if pad:
        rows.append(jnp.zeros((pad,) + x.shape[1:], F32))
    return jnp.concatenate(rows, 0).astype(BF16)


def radial_of(rb, w_stack):
    return mm(stack3(rb, "hhl"), w_stack, TN)


def orders_of(radial, h):
    c = h.shape[1]
    return [radial[:, q * c : (q + 1) * c] * h for q in range(3)]


def block_rows(ys, mask, q):
    lo, hi = ORDERS[q]
    return jnp.concatenate([ys[m] * mask for m in range(lo, hi)], 0)


def forward_cell(ys, mask, terms, a_ref, cell):
    slots = mask.shape[0]
    at = pl.ds(pl.multiple_of(cell * slots, slots), slots)
    for q, (lo, hi) in enumerate(ORDERS):
        sums = mm3(split(block_rows(ys, mask, q)), split(terms[q]), NN)
        for m in range(lo, hi):
            a_ref[m, at, :] = sums[(m - lo) * slots : (m - lo + 1) * slots]


def invariants_of(a_ref):
    a0 = a_ref[0]
    v = a_ref[1] * a_ref[1] + a_ref[2] * a_ref[2] + a_ref[3] * a_ref[3]
    t = a_ref[4] * a_ref[4]
    for m in range(5, 9):
        t = t + a_ref[m] * a_ref[m]
    return jnp.concatenate([a0, v, t], 1)


def a_grads(a_ref, d_update, mix, g_ref):
    c = d_update.shape[1]
    d_inv = mm3(split(d_update), split(mix), NT)
    for q, (lo, hi) in enumerate(ORDERS):
        part = d_inv[:, q * c : (q + 1) * c]
        for m in range(lo, hi):
            g_ref[m] = part if q == 0 else (2.0 * part) * a_ref[m]


def backward_cell(rb, ys, mask, radial, terms, h, g_ref, w_split, cell, want_dh):
    slots = mask.shape[0]
    c = h.shape[1]
    at = pl.ds(pl.multiple_of(cell * slots, slots), slots)
    d_y, pulls = [], []
    for q, (lo, hi) in enumerate(ORDERS):
        grads = jnp.concatenate([g_ref[m, at, :] for m in range(lo, hi)], 0)
        pulls.append(mm(stack3(block_rows(ys, mask, q), "hhl"), stack3(grads, "hlh"), TN))
        if q > 0:
            full = mm3(split(grads), split(terms[q]), NT)
            for m in range(hi - lo):
                d_y.append(jnp.sum(full[m * slots : (m + 1) * slots] * mask, 0, keepdims=True))
    z = jnp.concatenate([p * h for p in pulls], 1)
    d_rb = mm3(w_split, split(z), NT)
    zero = jnp.zeros_like(d_y[0])
    d_y = jnp.concatenate([zero] + d_y + [zero] * 7, 0)
    if not want_dh:
        return d_rb, d_y, None
    d_h = pulls[0] * radial[:, :c]
    for q in (1, 2):
        d_h = d_h + pulls[q] * radial[:, q * c : (q + 1) * c]
    return d_rb, d_y, d_h


def species_rows(geom, emb):
    s = emb.shape[0]
    row = iota((16, geom.shape[1]), 0).astype(F32)
    hot = jnp.where(row == geom[3:4], 1.0, 0.0).astype(BF16)
    table = jnp.concatenate([emb, jnp.zeros((16 - s, emb.shape[1]), F32)], 0)
    hi, lo = split(table)
    return mm(hot, hi, TN) + mm(hot, lo, TN)


def stencil_of(n):
    cell = n >> 3
    ox = ((cell * 57) >> 9) - 1
    row = (cell * 43) >> 7
    oy = row - 3 * (ox + 1) - 1
    oz = cell - 3 * row - 1
    return ox, oy, oz, n & 7


def ext_hot(n, rows, base, ye, ze):
    ox, oy, oz, slot = stencil_of(n)
    at = jnp.where(n < NO_EDGE, base + (ox * ye + oy) * ze + oz, -1)
    hot = jnp.where(iota((rows, n.shape[1]), 0) == at, 1.0, 0.0)
    return hot, slot


def expand_mat(slots, lanes):
    per = lanes // slots
    row, col = iota((lanes, 3 * lanes), 0), iota((lanes, 3 * lanes), 1)
    return jnp.where((col >= row * per) & (col < row * per + per), 1.0, 0.0).astype(F32)


def silu_parts(v):
    sig = 1.0 / (1.0 + jnp.exp(-v))
    return v * sig, sig * (1.0 + v * (1.0 - sig))


def first_kernel(dims, slots, edges, nb, ext_ref, own_ref, nbr_ref, emb_ref, h0_ref, w_ref, mix_ref,
                 geom_ref, hid_ref, a_ref, dsilu_ref, own_pos):
    X, Y, Z = dims
    ye, ze = Y + 2, Z + 2
    lanes = slots * edges
    rows = (X + 2) * ye * ze
    tab = ext_ref[...]
    hi = tab.astype(BF16).astype(F32)
    mid = (tab - hi).astype(BF16).astype(F32)
    low = tab - hi - mid
    parts = [p.astype(BF16) for p in (hi, mid, low)]
    own_pos[...] = lax.dot_general(
        own_ref[...], expand_mat(slots, lanes), (NN, ((), ())),
        precision=lax.Precision.HIGHEST, preferred_element_type=F32,
    )
    mask = slot_mask(slots, lanes)
    w_stack = stack3(w_ref[...], "hlh")
    s = edges ** (-0.5)

    def column(i, carry):
        cx, cy = i // Y, i % Y
        for cz in range(Z):
            cell = i * Z + cz
            n = nbr_ref[pl.ds(cell, 1), :]
            base = ((cx + 1) * ye + cy + 1) * ze + cz + 1
            hot, slot = ext_hot(n, rows, base, ye, ze)
            hot = hot.astype(BF16)
            got = mm(parts[0], hot, TN) + mm(parts[1], hot, TN) + mm(parts[2], hot, TN)
            pick = jnp.where(iota((slots, lanes), 0) == slot, 1.0, 0.0)
            vals = [
                jnp.sum(got[k * slots : (k + 1) * slots] * pick, 0, keepdims=True)
                for k in range(4)
            ]
            ox, oy, oz, _ = stencil_of(n)
            mine = own_pos[pl.ds(cell, 1), :]
            disp = [
                o.astype(F32) + vals[k] - mine[:, k * lanes : (k + 1) * lanes]
                for k, o in enumerate((ox, oy, oz))
            ]
            ms = jnp.where(n < NO_EDGE, s, 0.0)
            zero = jnp.zeros_like(ms)
            geom = jnp.concatenate(disp + [vals[3], ms, zero, zero, zero], 0)
            geom_ref[cell] = geom
            rb, ys, _ = basis(geom, nb)
            terms = orders_of(radial_of(rb, w_stack), species_rows(geom, emb_ref[...]))
            forward_cell(ys, mask, terms, a_ref, cell)
        return carry

    lax.fori_loop(0, X * Y, column, 0)
    v = mm3(split(invariants_of(a_ref)), split(mix_ref[...]), NN)
    up, slope = silu_parts(v)
    hid_ref[...] = h0_ref[...] + up
    dsilu_ref[...] = slope


def hot_rows(n, rows):
    return jnp.where(iota((rows, n.shape[1]), 0) == n, 1.0, 0.0).astype(BF16)


def second_kernel(dims, slots, edges, nb, ext_ref, geom_ref, nbr_ref, w_ref, mix_ref, read_ref,
                  energy_ref, dext_ref, drb_ref, dy_ref, a_ref, g_ref, h_ref):
    X, Y, Z = dims
    lanes = slots * edges
    c = ext_ref.shape[-1]
    mask = slot_mask(slots, lanes)
    w_stack = stack3(w_ref[...], "hlh")
    w_split = split(w_ref[...])
    near = 27 * slots
    pad = -near % 256

    def column(i, carry):
        cx, cy = i // Y, i % Y
        for cz in range(Z):
            cell = i * Z + cz
            table = jnp.concatenate(
                [
                    ext_ref[cx + a, cy + b, pl.ds(cz, 3)].reshape(3 * slots, c)
                    for a in range(3)
                    for b in range(3)
                ]
                + [jnp.zeros((pad, c), F32)],
                0,
            )
            hot = hot_rows(nbr_ref[pl.ds(cell, 1), :], near + pad)
            both = mm(hot, jnp.concatenate(split(table), 1), TN)
            h = both[:, :c] + both[:, c:]
            h_ref[pl.ds(pl.multiple_of(cell * lanes, lanes), lanes), :] = h
            rb, ys, _ = basis(geom_ref[cell], nb)
            terms = orders_of(radial_of(rb, w_stack), h)
            forward_cell(ys, mask, terms, a_ref, cell)
        return carry

    lax.fori_loop(0, X * Y, column, 0)
    v = mm3(split(invariants_of(a_ref)), split(mix_ref[...]), NN)
    up, slope = silu_parts(v)
    hid1 = ext_ref[1 : X + 1, 1 : Y + 1, 1 : Z + 1].reshape(X * Y * Z * slots, c)
    energy_ref[...] = jnp.sum((hid1 + up) * read_ref[...], 1, keepdims=True)
    a_grads(a_ref, slope * read_ref[...], mix_ref[...], g_ref)
    dext_ref[...] = jnp.zeros_like(dext_ref)

    def back(i, carry):
        cx, cy = i // Y, i % Y
        for cz in range(Z):
            cell = i * Z + cz
            h = h_ref[pl.ds(pl.multiple_of(cell * lanes, lanes), lanes), :]
            rb, ys, _ = basis(geom_ref[cell], nb)
            radial = radial_of(rb, w_stack)
            terms = orders_of(radial, h)
            d_rb, d_y, d_h = backward_cell(
                rb, ys, mask, radial, terms, h, g_ref, w_split, cell, True
            )
            drb_ref[cell] = d_rb
            dy_ref[cell] = d_y
            hot = hot_rows(nbr_ref[pl.ds(cell, 1), :], near + pad)
            both = mm(hot, jnp.concatenate(split(d_h), 1), NN)
            sums = both[:, :c] + both[:, c:]
            for j, (a, b) in enumerate(itertools.product(range(3), repeat=2)):
                at = (cx + a, cy + b, pl.ds(cz, 3))
                part = sums[j * 3 * slots : (j + 1) * 3 * slots].reshape(3, slots, c)
                dext_ref[at] = dext_ref[at] + part
        return carry

    lax.fori_loop(0, X * Y, back, 0)


def third_kernel(dims, slots, edges, nb, dh_ref, a_ref, dsilu_ref, geom_ref, nbr_ref, drb_ref, dy_ref,
                 emb_ref, w_ref, mix_ref, read_ref, sent_ref, got_ref, g_ref, eg_ref):
    X, Y, Z = dims
    ye, ze = Y + 2, Z + 2
    lanes = slots * edges
    rows = (X + 2) * ye * ze
    mask = slot_mask(slots, lanes)
    w_stack = stack3(w_ref[...], "hlh")
    w_split = split(w_ref[...])
    a_grads(a_ref, dsilu_ref[...] * (dh_ref[...] + read_ref[...]), mix_ref[...], g_ref)
    sent_ref[...] = jnp.zeros_like(sent_ref)

    def back(i, carry):
        cx, cy = i // Y, i % Y
        for cz in range(Z):
            cell = i * Z + cz
            geom = geom_ref[cell]
            rb, ys, extra = basis(geom, nb)
            h = species_rows(geom, emb_ref[...])
            radial = radial_of(rb, w_stack)
            terms = orders_of(radial, h)
            d_rb, d_y, _ = backward_cell(
                rb, ys, mask, radial, terms, h, g_ref, w_split, cell, False
            )
            grads = geom_pull(geom, extra, d_rb + drb_ref[cell], d_y + dy_ref[cell])
            eg_ref[pl.ds(cell, 1), :] = jnp.concatenate(grads, 1)
            n = nbr_ref[pl.ds(cell, 1), :]
            base = ((cx + 1) * ye + cy + 1) * ze + cz + 1
            hot, slot = ext_hot(n, rows, base, ye, ze)
            hot = hot.astype(BF16)
            pick = jnp.where(iota((slots, lanes), 0) == slot, 1.0, 0.0)
            x = jnp.concatenate([g * pick for g in grads] + [jnp.zeros((lanes - 3 * slots, lanes), F32)], 0)
            hi, lo = split(x)
            sent_ref[...] += mm(hot, hi, NT) + mm(hot, lo, NT)
        return carry

    lax.fori_loop(0, X * Y, back, 0)
    got_ref[...] = lax.dot_general(
        eg_ref[...], expand_mat(slots, lanes), (NT, ((), ())),
        precision=lax.Precision.HIGHEST, preferred_element_type=F32,
    )


def call(body, outs, scratch, name, *args):
    return pl.pallas_call(
        body,
        out_shape=[jax.ShapeDtypeStruct(s, F32) for s in outs],
        in_specs=[VM] * len(args),
        out_specs=[VM] * len(outs),
        scratch_shapes=[pltpu.VMEM(s, F32) for s in scratch],
        compiler_params=pltpu.CompilerParams(vmem_limit_bytes=56 * 1024 * 1024),
        name=name,
    )(*args)


def shards(positions, species, neighbors, edge_mask, species_embed, radial_weight, mix_weight, readout, energy_offset):
    X, Y, Z, slots, edges = neighbors.shape
    dims = (X, Y, Z)
    cells = X * Y * Z
    atoms = cells * slots
    lanes = slots * edges
    c = species_embed.shape[1]
    nb = radial_weight.shape[1]
    ext = (X + 2, Y + 2, Z + 2)
    rows = ext[0] * ext[1] * ext[2]

    nbr = jnp.where(edge_mask != 0, neighbors, NO_EDGE).reshape(cells, lanes)
    four = jnp.concatenate([positions, species[..., None].astype(F32)], -1)
    own_tab = jnp.swapaxes(four, -1, -2).reshape(cells, 4 * slots)
    own_tab = jnp.pad(own_tab, ((0, 0), (0, lanes - 4 * slots)))
    ext_tab = spread(own_tab.reshape(X, Y, Z, 1, lanes), 1).reshape(rows, lanes)
    flat_species = species.reshape(atoms, 1)
    h0 = jnp.zeros((atoms, c), F32)
    offset = jnp.zeros((atoms, 1), F32)
    for s in range(species_embed.shape[0]):
        h0 = jnp.where(flat_species == s, species_embed[s], h0)
        offset = jnp.where(flat_species == s, energy_offset[s], offset)
    size = (dims, slots, edges, nb)
    read = readout.reshape(1, c)
    geom, hid1, a0, dsilu = call(
        functools.partial(first_kernel, *size),
        [(cells, 8, lanes), (atoms, c), (9, atoms, c), (atoms, c)],
        [(cells, 3 * lanes)],
        "first",
        ext_tab, own_tab, nbr, species_embed, h0, radial_weight[0], mix_weight[0],
    )
    hid_ext = spread(hid1.reshape(X, Y, Z, slots, c), 2)
    energy, d_ext, d_rb, d_y = call(
        functools.partial(second_kernel, *size),
        [(atoms, 1), ext + (slots, c), (cells, nb, lanes), (cells, 16, lanes)],
        [(9, atoms, c), (9, atoms, c), (cells * lanes, c)],
        "second",
        hid_ext, geom, nbr, radial_weight[1], mix_weight[1], read,
    )
    d_h = fold(d_ext, 3).reshape(atoms, c)
    sent, got = call(
        functools.partial(third_kernel, *size),
        [(rows, lanes), (cells, lanes)],
        [(9, atoms, c), (cells, 3 * lanes)],
        "third",
        d_h, a0, dsilu, geom, nbr, d_rb, d_y, species_embed, radial_weight[0], mix_weight[0], read,
    )
    back = fold(sent.reshape(ext + (1, lanes)), 4).reshape(cells, lanes)
    forces = (got - back)[:, : 3 * slots].reshape(X, Y, Z, 3, slots)
    energy = energy + offset
    return energy.reshape(X, Y, Z, slots), jnp.swapaxes(forces, -1, -2)


def solution(mesh):
    g = P("gx", "gy", "gz")
    return jax.shard_map(
        shards,
        mesh=mesh,
        in_specs=(g, g, g, g, P(), P(), P(), P(), P()),
        out_specs=(g, g),
        check_vma=False,
    )
```

profile of v0, /device:TPU:0, one launch (start us, length us, event | category | flops | bytes accessed | tf_op | source)
XLA Modules:
  0.0 131.0 jit_solution(6550884397347493201)
XLA Ops:
  0.6 0.0 copy-start.1
  0.6 0.0 copy-start.3
  0.7 0.0 copy-start.2
  0.7 1.4 %fusion = (f32[1]{0:T(128)}, f32[1]{0:T(128)}, f32[1]{0:T(128)}, f32[1]{0:T(128)}) fusion(f32[4]{0:T(128)} %param.17), kind=kLoop, calls=%fused_computation.19 | loop fusion | bytes 32 | tf_op jit(solution)/shard_map/slice | solution.py:525
  2.1 3.3 %select_select_fusion.1 = (f32[2,4,4,8]{3,2,1,0:T(4,128)S(1)}, pred[2,4,4,8]{3,2,1,0:T(4,128)(4,1)S(1)}, pred[2,4,4,8]{3,2,1,0:T(4,128)(4,1)S(1)}, pred[2,4,4,8]{3,2,1,0:T(4,128)(4,1)S(1)}, pred[2,4,4,8]{3,2,1,0:T(4,128)(4,1)S(1)}) fusion(f32[]{:T(128)} %bitcast.16, f32[]{:T(128)} %bitcast.19, f32[]{:T(128)} %bitcast.18, f32[]{:T(128)} %bitcast.17, ...), kind=kLoop, calls=%fused_computation.7 | loop fusion | flops 2048 | bytes 3088 | tf_op jit(solution)/shard_map/jit(_where)/select_n | solution.py:525
  5.4 0.1 eq.79
  5.5 0.1 eq.81
  5.6 0.1 eq.83
  5.7 0.1 eq.85
  5.8 0.8 slice_bitcast_fusion.7
  6.6 0.9 select_select_fusion.h0_ref
  7.5 1.8 %slice_bitcast_fusion = (f32[384,128]{1,0:T(8,128)}, f32[384,128]{1,0:T(8,128)}) fusion(f32[2,384,128]{2,1,0:T(8,128)} %param.15), kind=kLoop, calls=%fused_computation | loop fusion | bytes 786432 | tf_op jit(solution)/shard_map/squeeze | solution.py:541
  9.3 1.0 compare_select_fusion
  10.3 0.7 reshape.141.nbr_ref
  11.0 0.0 copy-done.3
  11.0 0.6 slice_bitcast_fusion.2
  11.6 0.0 copy-done.1
  11.6 0.0 copy-done.2
  11.7 0.1 reshape.138
  11.8 0.6 pad.4.own_ref
  12.4 11.2 %spread_1.1 = f32[4,6,6,1,128]{4,3,2,1,0:T(1,128)} custom-call(f32[2,4,4,1,128]{4,3,2,1,0:T(1,128)} %bitcast.41), custom_call_target="tpu_custom_call" | custom-call | tf_op jit(solution)/shard_map/spread_1/pallas_call | solution.py:105
  23.6 22.1 %first.1 = (f32[32,8,128]{2,1,0:T(8,128)}, f32[256,128]{1,0:T(8,128)}, f32[9,256,128]{2,1,0:T(8,128)}, f32[256,128]{1,0:T(8,128)}) custom-call(f32[144,128]{1,0:T(8,128)} %bitcast.39, f32[32,128]{1,0:T(8,128)} %pad.4.own_ref, s32[32,128]{1,0:T(8,128)} %reshape.141.nbr_ref, f32[4,128]{1,0:T(4,128)} %emb_ref.3, f32[256,128]{1,0:T(8,128)} %select_select_fusion.h0_ref, ...), custom_call_target="tpu_custom_call" | custom-call | tf_op jit(solution)/shard_map/first/pallas_call | solution.py:493
  45.6 12.4 %spread_2.1.ext_ref = f32[4,6,6,8,128]{4,3,2,1,0:T(8,128)} custom-call(f32[2,4,4,8,128]{4,3,2,1,0:T(8,128)} %bitcast.42), custom_call_target="tpu_custom_call" | custom-call | tf_op jit(solution)/shard_map/spread_2/pallas_call | solution.py:105
  58.1 26.3 %second.1 = (f32[256,1]{1,0:T(8,128)}, f32[4,6,6,8,128]{4,3,2,1,0:T(8,128)}, f32[32,8,128]{2,1,0:T(8,128)}, f32[32,16,128]{2,1,0:T(8,128)}) custom-call(f32[4,6,6,8,128]{4,3,2,1,0:T(8,128)} %spread_2.1.ext_ref, f32[32,8,128]{2,1,0:T(8,128)} %get-tuple-element.13.geom_ref, s32[32,128]{1,0:T(8,128)} %reshape.141.nbr_ref, f32[8,384]{1,0:T(8,128)} %get-tuple-element.31.w_ref, ...), custom_call_target="tpu_custom_call" | custom-call | tf_op jit(solution)/shard_map/second/pallas_call | solution.py:493
  84.4 13.4 %fold_3.1 = f32[2,4,4,8,128]{4,3,2,1,0:T(8,128)} custom-call(f32[4,6,6,8,128]{4,3,2,1,0:T(8,128)} %get-tuple-element.15.ext_ref), custom_call_target="tpu_custom_call" | custom-call | tf_op jit(solution)/shard_map/fold_3/pallas_call | solution.py:145
  97.8 0.0 copy-start
  97.8 21.5 %third.1 = (f32[144,128]{1,0:T(8,128)}, f32[32,128]{1,0:T(8,128)}) custom-call(f32[256,128]{1,0:T(8,128)} %bitcast.38, f32[9,256,128]{2,1,0:T(8,128)} %get-tuple-element.16.a_ref, f32[256,128]{1,0:T(8,128)} %get-tuple-element.17.dsilu_ref, f32[32,8,128]{2,1,0:T(8,128)} %get-tuple-element.13.geom_ref, s32[32,128]{1,0:T(8,128)} %reshape.141.nbr_ref, ...), custom_call_target="tpu_custom_call" | custom-call | tf_op jit(solution)/shard_map/third/pallas_call | solution.py:493
  119.2 9.3 %fold_4.1 = f32[2,4,4,1,128]{4,3,2,1,0:T(1,128)} custom-call(f32[4,6,6,1,128]{4,3,2,1,0:T(1,128)} %bitcast.43), custom_call_target="tpu_custom_call" | custom-call | tf_op jit(solution)/shard_map/fold_4/pallas_call | solution.py:145
  128.6 0.7 slice_subtract_fusion
  129.3 0.1 reshape.148
  129.4 0.6 copy.19
  130.1 0.1 reshape.151
  130.2 0.0 copy-done
  130.2 0.1 add_reduce_fusion
  130.3 0.7 reshape.144
  (3 shorter events, 0.0 us)
Async XLA Ops:
  0.6 11.0 %copy-start.1 = (s32[2,4,4,8]{3,2,1,0:T(4,128)S(1)}, s32[2,4,4,8]{3,2,1,0:T(4,128)}, u32[]{:S(2)}) copy-start(s32[2,4,4,8]{3,2,1,0:T(4,128)} %param.10) | copy-start | bytes 3076
  0.6 10.3 %copy-start.3 = (f32[2,8,384]{2,1,0:T(8,128)S(1)}, f32[2,8,384]{2,1,0:T(8,128)}, u32[]{:S(2)}) copy-start(f32[2,8,384]{2,1,0:T(8,128)} %param.14) | copy-start | bytes 73732
  0.7 10.9 %copy-start.2 = (f32[2,4,4,8,3]{3,2,4,1,0:T(4,128)S(1)}, f32[2,4,4,8,3]{3,2,4,1,0:T(4,128)}, u32[]{:S(2)}) copy-start(f32[2,4,4,8,3]{3,2,4,1,0:T(4,128)} %param.9) | copy-start | bytes 9220
  97.8 32.4 %copy-start = (f32[256,1]{1,0:T(8,128)S(1)}, f32[256,1]{1,0:T(8,128)}, u32[]{:S(2)}) copy-start(f32[256,1]{1,0:T(8,128)} %get-tuple-element.14) | copy-start | bytes 3076
where the time goes:
time: 132 us; the launch traced here: 131 us
  Pallas kernels  116 us (88%)
  local copies, waits for them, and re-layouts  8.06 us (6%)
  other arithmetic  6.01 us (5%)
    pallas_call x3, Pallas kernels, call(): pl.pallas_call(body, out_shape=[jax.ShapeDtypeStruct(s, F32) for s in out...  69.9 us
    pallas_call x2, Pallas kernels, spread(): pl.pallas_call(functools.partial(spread_kernel, dims), out_shape=jax.Shap...  23.6 us
    pallas_call x2, Pallas kernels, fold(): pl.pallas_call(functools.partial(fold_kernel, dims), out_shape=jax.ShapeD...  22.7 us
    select_n x1, other arithmetic, shards(): offset = jnp.where(flat_species == s, energy_offset[s], offset)  3.29 us

commit v1 on v0

v1 whole, which is shorter than its diff:
```python
import functools
import itertools
import math

import jax
import jax.numpy as jnp
from jax import lax
from jax.experimental import pallas as pl
from jax.experimental.pallas import tpu as pltpu
from jax.sharding import PartitionSpec as P

F32 = jnp.float32
BF16 = jnp.bfloat16
MESH = pl.DeviceIdType.MESH
AXES = ("gx", "gy", "gz")
RC = 2.0
NO_EDGE = 1023
OFFSETS = [o for o in itertools.product((-1, 0, 1), repeat=3) if any(o)]
ORDERS = ((0, 1), (1, 4), (4, 9))
VM = pl.BlockSpec(memory_space=pltpu.VMEM)

NN = ((1,), (0,))
NT = ((1,), (1,))
TN = ((0,), (0,))


def split(x):
    hi = x.astype(BF16)
    return hi, (x - hi.astype(F32)).astype(BF16)


def split32(x):
    hi = x.astype(BF16).astype(F32)
    return hi, x - hi


def mm(a, b, dims):
    return lax.dot_general(a, b, (dims, ((), ())), preferred_element_type=F32)


def mm3(a, b, dims):
    return mm(a[0], b[0], dims) + (mm(a[0], b[1], dims) + mm(a[1], b[0], dims))


def peer(o):
    ids = []
    for axis, step in zip(AXES, o):
        n = lax.axis_size(axis)
        ids.append(lax.rem(lax.axis_index(axis) + (step + n), n))
    return tuple(ids)


def greet():
    barrier = pltpu.get_barrier_semaphore()
    for o in OFFSETS:
        pl.semaphore_signal(barrier, inc=1, device_id=peer(o), device_id_type=MESH)
    pl.semaphore_wait(barrier, len(OFFSETS))


def box(o, dims, minus, zero, plus):
    out = []
    for s, n in zip(o, dims):
        out.append(zero(n) if s == 0 else (plus(n) if s > 0 else minus(n)))
    return tuple(out)


def face(o, dims):
    return box(o, dims, lambda n: pl.ds(0, 1), lambda n: pl.ds(0, n), lambda n: pl.ds(n - 1, 1))


def halo(o, dims):
    return box(o, dims, lambda n: pl.ds(0, 1), lambda n: pl.ds(1, n), lambda n: pl.ds(n + 1, 1))


def opposite(o):
    return tuple(-s for s in o)


def iota(shape, dim):
    return lax.broadcasted_iota(jnp.int32, shape, dim)


def slot_mask(slots, lanes):
    per = lanes // slots
    lane, row = iota((slots, lanes), 1), iota((slots, lanes), 0)
    return jnp.where((lane >= row * per) & (lane < row * per + per), 1.0, 0.0).astype(F32)


def basis(geom, nb):
    dx, dy, dz, ms = geom[0:1], geom[1:2], geom[2:3], geom[4:5]
    r2 = dx * dx + dy * dy + dz * dz
    r = jnp.sqrt(r2)
    inside = r < RC
    w = 1.0 - r2 * (1.0 / RC**2)
    u = jnp.where(inside, w * w, 0.0)
    mu = iota((nb, geom.shape[1]), 0).astype(F32) * (RC / (nb - 1))
    g = ((nb - 1) / RC) ** 2
    off = r - mu
    gauss = jnp.exp(-g * off * off)
    rb = gauss * u
    px, py, pz = dx / RC, dy / RC, dz / RC
    c3, c5, c15 = math.sqrt(3.0), math.sqrt(5.0), math.sqrt(15.0)
    ys = [
        ms,
        ms * (c3 * px),
        ms * (c3 * py),
        ms * (c3 * pz),
        ms * (c15 * px * py),
        ms * (c15 * py * pz),
        ms * ((0.5 * c5) * (3.0 * pz * pz - (px * px + py * py + pz * pz))),
        ms * (c15 * px * pz),
        ms * ((0.5 * c15) * (px * px - py * py)),
    ]
    return rb, ys, (r, w, inside, gauss, off, g, (px, py, pz))


def geom_pull(geom, extra, d_rb, d_y):
    r, w, inside, gauss, off, g, (px, py, pz) = extra
    ms = geom[4:5]
    du = jnp.where(inside, -r * w, 0.0)
    u = jnp.where(inside, w * w, 0.0)
    d_r = jnp.sum(d_rb * gauss * (du - 2.0 * g * off * u), 0, keepdims=True)
    c3, c5, c15 = math.sqrt(3.0), math.sqrt(5.0), math.sqrt(15.0)
    gy = [ms * d_y[m : m + 1] for m in range(9)]
    vx = c3 * gy[1] + c15 * (py * gy[4] + pz * gy[7] + px * gy[8]) - c5 * px * gy[6]
    vy = c3 * gy[2] + c15 * (px * gy[4] + pz * gy[5] - py * gy[8]) - c5 * py * gy[6]
    vz = c3 * gy[3] + c15 * (py * gy[5] + px * gy[7]) + 2.0 * c5 * pz * gy[6]
    k = d_r / jnp.maximum(r, 1e-20)
    return [v / RC + k * geom[i : i + 1] for i, v in enumerate((vx, vy, vz))]


def stack3(x, order):
    hi, lo = split32(x)
    parts = {"h": hi, "l": lo}
    rows = [parts[o] for o in order]
    pad = -(3 * x.shape[0]) % 16
    if pad:
        rows.append(jnp.zeros((pad,) + x.shape[1:], F32))
    return jnp.concatenate(rows, 0).astype(BF16)


def invariants_of(a_ref):
    a0 = a_ref[0]
    v = a_ref[1] * a_ref[1] + a_ref[2] * a_ref[2] + a_ref[3] * a_ref[3]
    t = a_ref[4] * a_ref[4]
    for m in range(5, 9):
        t = t + a_ref[m] * a_ref[m]
    return jnp.concatenate([a0, v, t], 1)


def a_grads(a_ref, d_update, mix, g_ref):
    c = d_update.shape[1]
    d_inv = mm3(split(d_update), split(mix), NT)
    for q, (lo, hi) in enumerate(ORDERS):
        part = d_inv[:, q * c : (q + 1) * c]
        for m in range(lo, hi):
            g_ref[m] = part if q == 0 else (2.0 * part) * a_ref[m]


def stencil_of(n):
    cell = n >> 3
    ox = ((cell * 57) >> 9) - 1
    row = (cell * 43) >> 7
    oy = row - 3 * (ox + 1) - 1
    oz = cell - 3 * row - 1
    return ox, oy, oz, n & 7


def ext_hot(n, rows, base, ye, ze):
    ox, oy, oz, slot = stencil_of(n)
    at = jnp.where(n < NO_EDGE, base + (ox * ye + oy) * ze + oz, -1)
    hot = jnp.where(iota((rows, n.shape[1]), 0) == at, 1.0, 0.0)
    return hot, slot


def expand_mat(slots, lanes):
    per = lanes // slots
    row, col = iota((lanes, 3 * lanes), 0), iota((lanes, 3 * lanes), 1)
    return jnp.where((col >= row * per) & (col < row * per + per), 1.0, 0.0).astype(F32)


def silu_parts(v):
    sig = 1.0 / (1.0 + jnp.exp(-v))
    return v * sig, sig * (1.0 + v * (1.0 - sig))


def hot_rows(n, rows):
    return jnp.where(iota((rows, n.shape[1]), 0) == n, 1.0, 0.0).astype(BF16)


def radial_of(rb, w_stack):
    return mm(stack3(rb, "hhl"), w_stack, TN)


def rows_hl(x):
    hi, lo = split32(x)
    return jnp.concatenate([hi, lo], 0).astype(BF16)


def order_rows(ys, mask, q):
    lo, hi = ORDERS[q]
    return jnp.concatenate([ys[m] * mask for m in range(lo, hi)], 0)


def exchange(src, dst, src_at, dst_at, send_sem, recv_sem, base):
    copies = []
    for i, o in enumerate(OFFSETS):
        copies.append(
            pltpu.make_async_remote_copy(
                src_ref=src.at[src_at(o)],
                dst_ref=dst.at[dst_at(o)],
                send_sem=send_sem.at[base + i],
                recv_sem=recv_sem.at[base + i],
                device_id=peer(o),
                device_id_type=MESH,
            )
        )
        copies[-1].start()
    return copies


def kernel(dims, slots, edges, nb, own5_ref, own_ref, nbr_ref, spec_ref, emb_ref, w_ref, mix_ref, read_ref,
           off_ref, energy_ref, force_ref,
           tab_ext, tab2, own_pos, hot_ref, hotx_ref, geom_ref, ym_ref, we_ref, v_ref, a_ref, g_ref,
           dsilu_ref, hid_own, hid_ext, rad_ref, h_ref, t_ref, z_ref, dext, drecv, drb_ref, dy_ref,
           dh_ref, eg_ref, sent, sent5, srecv, fold5, send_sem, recv_sem, local_sem):
    X, Y, Z = dims
    cells = X * Y * Z
    atoms = cells * slots
    ye, ze = Y + 2, Z + 2
    rows = (X + 2) * ye * ze
    lanes = slots * edges
    c = mix_ref.shape[-1]
    ns = emb_ref.shape[0]
    near = 27 * slots
    near_pad = hot_ref.shape[1]
    n_o = len(OFFSETS)
    s = edges ** (-0.5)
    mask = slot_mask(slots, lanes)
    own_face = lambda o: face(o, dims)
    own_in = lambda o: halo(opposite(o), dims)
    ext_face = lambda o: halo(o, dims)
    inner = tuple(pl.ds(1, n) for n in dims)
    grid = list(itertools.product(*[range(d + 2) for d in dims]))

    barrier = pltpu.get_barrier_semaphore()
    for o in OFFSETS:
        pl.semaphore_signal(barrier, inc=1, device_id=peer(o), device_id_type=MESH)

    def base_of(cx, cy, cz):
        return ((cx + 1) * ye + cy + 1) * ze + cz + 1

    def loop(body):
        def step(i, carry):
            cx, cy = i // Y, i % Y
            body(i, cx, cy)
            return carry
        lax.fori_loop(0, X * Y, step, 0)

    def edge_rows(cell):
        return pl.ds(pl.multiple_of(cell * lanes, lanes), lanes)

    def atom_rows(cell):
        return pl.ds(pl.multiple_of(cell * slots, slots), slots)

    def build_hot(i, cx, cy):
        for cz in range(Z):
            cell = i * Z + cz
            n = nbr_ref[pl.ds(cell, 1), :]
            hot_ref[cell] = hot_rows(n, near_pad)
            hotx_ref[cell] = ext_hot(n, rows, base_of(cx, cy, cz), ye, ze)[0].astype(BF16)

    loop(build_hot)
    pl.semaphore_wait(barrier, n_o)

    local = pltpu.make_async_copy(own5_ref, tab_ext.at[inner], local_sem.at[0])
    local.start()
    copies = exchange(own5_ref, tab_ext, own_face, own_in, send_sem, recv_sem, 0)
    own_pos[...] = lax.dot_general(
        own_ref[...], expand_mat(slots, lanes), (NN, ((), ())),
        precision=lax.Precision.HIGHEST, preferred_element_type=F32,
    )
    emb = emb_ref[...]
    for k in range(ns):
        wide = jnp.concatenate([emb[k : k + 1]] * 3, 1)
        we_ref[k * nb : (k + 1) * nb, :] = w_ref[0] * wide
    spec_row = spec_ref[...]
    spec_hot = jnp.where(iota((16, atoms), 0) == spec_row, 1.0, 0.0).astype(BF16)
    emb_hi, emb_lo = split(jnp.concatenate([emb, jnp.zeros((16 - ns, c), F32)], 0))
    h0 = mm(spec_hot, emb_hi, TN) + mm(spec_hot, emb_lo, TN)
    eye = jnp.where(iota((4 * slots, lanes), 0) == iota((4 * slots, lanes), 1), 1.0, 0.0).astype(BF16)
    local.wait()
    for copy in copies:
        copy.wait()

    for r, at in enumerate(grid):
        tab2[r : r + 1, :] = tab_ext[at]
    tab = tab2[...]
    hi, rest = split32(tab)
    mid, low = split32(rest)
    tab_t = jnp.concatenate([mm(eye, p.astype(BF16), NT) for p in (hi, mid, low)], 0).astype(BF16)

    def rb_species(rb, geom):
        return jnp.concatenate([jnp.where(geom[3:4] == float(k), rb, 0.0) for k in range(ns)], 0)

    def layer0(i, cx, cy):
        for cz in range(Z):
            cell = i * Z + cz
            n = nbr_ref[pl.ds(cell, 1), :]
            got = mm(tab_t, hotx_ref[cell], NN)
            got = got[: 4 * slots] + got[4 * slots : 8 * slots] + got[8 * slots :]
            ox, oy, oz, slot = stencil_of(n)
            pick = iota((slots, lanes), 0) == slot
            vals = [
                jnp.sum(jnp.where(pick, got[k * slots : (k + 1) * slots], 0.0), 0, keepdims=True)
                for k in range(4)
            ]
            mine = own_pos[pl.ds(cell, 1), :]
            disp = [
                o.astype(F32) + vals[k] - mine[:, k * lanes : (k + 1) * lanes]
                for k, o in enumerate((ox, oy, oz))
            ]
            ms = jnp.where(n < NO_EDGE, s, 0.0)
            zero = jnp.zeros_like(ms)
            geom = jnp.concatenate(disp + [vals[3], ms, zero, zero, zero], 0)
            geom_ref[cell] = geom
            rb, ys, _ = basis(geom, nb)
            blocks = [rows_hl(order_rows(ys, mask, q)) for q in range(3)]
            ym = jnp.concatenate(blocks, 0)
            ym_ref[cell] = ym
            rbs = rb_species(rb, geom)
            v = mm(ym, rows_hl(rbs), NT)
            w = ns * nb
            v = v[:, :w] + v[:, w : 2 * w]
            at = 0
            for lo, hi in ORDERS:
                span = (hi - lo) * slots
                part = v[at : at + span] + v[at + span : at + 2 * span]
                at += 2 * span
                for m in range(lo, hi):
                    v_ref[m, atom_rows(cell), :] = part[(m - lo) * slots : (m - lo + 1) * slots]

    loop(layer0)
    for q, (lo, hi) in enumerate(ORDERS):
        part = split(we_ref[:, q * c : (q + 1) * c])
        for m in range(lo, hi):
            a_ref[0, m] = mm3(split(v_ref[m]), part, NN)
    v = mm3(split(invariants_of(a_ref.at[0])), split(mix_ref[0]), NN)
    up, slope = silu_parts(v)
    dsilu_ref[...] = slope
    hid1 = h0 + up
    hid_own[...] = hid1.reshape(X, Y, Z, slots, c)
    local = pltpu.make_async_copy(hid_own, hid_ext.at[inner], local_sem.at[1])
    local.start()
    copies = exchange(hid_own, hid_ext, own_face, own_in, send_sem, recv_sem, n_o)

    w1 = w_ref[1]
    w_stack = stack3(w1, "hlh")

    def radials(i, cx, cy):
        for cz in range(Z):
            cell = i * Z + cz
            rb, _, _ = basis(geom_ref[cell], nb)
            rad_ref[edge_rows(cell), :] = radial_of(rb, w_stack)

    loop(radials)
    local.wait()
    for copy in copies:
        copy.wait()

    def layer1(i, cx, cy):
        for cz in range(Z):
            cell = i * Z + cz
            table = jnp.concatenate(
                [
                    hid_ext[cx + a, cy + b, pl.ds(cz, 3)].reshape(3 * slots, c)
                    for a in range(3)
                    for b in range(3)
                ]
                + [jnp.zeros((near_pad - near, c), F32)],
                0,
            )
            both = mm(hot_ref[cell], jnp.concatenate(split(table), 1), TN)
            h = both[:, :c] + both[:, c:]
            h_ref[edge_rows(cell), :] = h
            ym = ym_ref[cell]
            at = 0
            for q, (lo, hi) in enumerate(ORDERS):
                t = rad_ref[edge_rows(cell), q * c : (q + 1) * c] * h
                t_hi, t_lo = split(t)
                t_ref[cell, q, :lanes, :] = t_hi
                t_ref[cell, q, lanes:, :] = t_lo
                span = (hi - lo) * slots
                sums = mm(ym[at : at + 2 * span], jnp.concatenate([t_hi, t_lo], 1), NN)
                at += 2 * span
                sums = sums[:, :c] + sums[:, c:]
                sums = sums[:span] + sums[span:]
                for m in range(lo, hi):
                    a_ref[1, m, atom_rows(cell), :] = sums[(m - lo) * slots : (m - lo + 1) * slots]

    loop(layer1)
    read = read_ref[...]
    v = mm3(split(invariants_of(a_ref.at[1])), split(mix_ref[1]), NN)
    up, slope = silu_parts(v)
    a_grads(a_ref.at[1], slope * read, mix_ref[1], g_ref)
    dext[...] = jnp.zeros_like(dext)

    def back1(i, cx, cy):
        for cz in range(Z):
            cell = i * Z + cz
            h = h_ref[edge_rows(cell), :]
            ym = ym_ref[cell]
            d_h = None
            at = 0
            for q, (lo, hi) in enumerate(ORDERS):
                span = (hi - lo) * slots
                grads = jnp.concatenate([g_ref[m, atom_rows(cell), :] for m in range(lo, hi)], 0)
                g_hi, g_lo = split32(grads)
                yq = ym[at : at + 2 * span]
                at += 2 * span
                lhs = jnp.concatenate([yq, yq], 0)
                rhs = jnp.concatenate([g_hi, g_hi, g_lo, g_lo], 0).astype(BF16)
                pull = mm(lhs, rhs, TN)
                term = pull * rad_ref[edge_rows(cell), q * c : (q + 1) * c]
                d_h = term if d_h is None else d_h + term
                z_hi, z_lo = split(pull * h)
                z_ref[cell, :lanes, q * c : (q + 1) * c] = z_hi
                z_ref[cell, lanes:, q * c : (q + 1) * c] = z_lo
            both = mm(hot_ref[cell], jnp.concatenate(split(d_h), 1), NN)
            sums = both[:, :c] + both[:, c:]
            for j, (a, b) in enumerate(itertools.product(range(3), repeat=2)):
                at = (cx + a, cy + b, pl.ds(cz, 3))
                part = sums[j * 3 * slots : (j + 1) * 3 * slots].reshape(3, slots, c)
                dext[at] = dext[at] + part

    loop(back1)
    copies = exchange(dext, drecv, ext_face, ext_face, send_sem, recv_sem, 2 * n_o)

    hid2 = hid_ext[1 : X + 1, 1 : Y + 1, 1 : Z + 1].reshape(atoms, c) + up
    read8 = jnp.concatenate([read] * 8, 0)
    energy = mm3(split(read8), split(hid2), NT)[0:1]
    for k in range(ns):
        energy = energy + jnp.where(spec_row == k, off_ref[0, k], 0.0)
    energy_ref[...] = energy
    w_rows = rows_hl(w1)

    def pull_rows(full, first, count):
        return [
            jnp.sum(full[m * slots : (m + 1) * slots] * mask, 0, keepdims=True)
            for m in range(first, first + count)
        ]

    def geom1(i, cx, cy):
        for cz in range(Z):
            cell = i * Z + cz
            d = mm(w_rows, z_ref[cell], NT)
            d = d[:, :lanes] + d[:, lanes:]
            drb_ref[cell] = d[:nb] + d[nb:]
            d_y = [jnp.zeros((1, lanes), F32)]
            for q in (1, 2):
                lo, hi = ORDERS[q]
                grads = jnp.concatenate([g_ref[m, atom_rows(cell), :] for m in range(lo, hi)], 0)
                full = mm(rows_hl(grads), t_ref[cell, q], NT)
                full = full[:, :lanes] + full[:, lanes:]
                span = (hi - lo) * slots
                d_y += pull_rows(full[:span] + full[span:], 0, hi - lo)
            dy_ref[cell] = jnp.concatenate(d_y + [d_y[0]] * 7, 0)

    loop(geom1)
    dh_ref[...] = dext[inner]
    for o, copy in zip(OFFSETS, copies):
        copy.wait()
        at = face(opposite(o), dims)
        dh_ref[at] = dh_ref[at] + drecv[halo(o, dims)]

    cot = dh_ref[...].reshape(atoms, c) + read
    a_grads(a_ref.at[0], dsilu_ref[...] * cot, mix_ref[0], g_ref)
    for q, (lo, hi) in enumerate(ORDERS):
        part = split(we_ref[:, q * c : (q + 1) * c])
        for m in range(lo, hi):
            v_ref[m] = mm3(split(g_ref[m]), part, NT)
    sent[...] = jnp.zeros_like(sent)

    def back0(i, cx, cy):
        hots, xs = [], []
        for cz in range(Z):
            cell = i * Z + cz
            geom = geom_ref[cell]
            rb, ys, extra = basis(geom, nb)
            rbs = rb_species(rb, geom)
            d_v = jnp.concatenate([v_ref[m, atom_rows(cell), :] for m in range(9)], 0)
            d_v = split32(d_v)
            r_v = split32(rbs)
            lhs = jnp.concatenate([d_v[0], d_v[1]], 0).astype(BF16)
            rhs = jnp.concatenate([r_v[0], r_v[1]], 1).astype(BF16)
            full = mm(lhs, rhs, NN)
            full = full[:, :lanes] + full[:, lanes:]
            full = full[: 9 * slots] + full[9 * slots :]
            d_y = [jnp.zeros((1, lanes), F32)] + pull_rows(full, 1, 8)
            yall = jnp.concatenate([y * mask for y in ys], 0)
            d_rbs = mm(
                jnp.concatenate([d_v[0], d_v[0], d_v[1], jnp.zeros((slots, ns * nb), F32)], 0).astype(BF16),
                stack3(yall, "hlh"),
                TN,
            )
            d_rb = drb_ref[cell]
            for k in range(ns):
                d_rb = d_rb + jnp.where(geom[3:4] == float(k), d_rbs[k * nb : (k + 1) * nb], 0.0)
            d_y = jnp.concatenate(d_y + [d_y[0]] * 7, 0) + dy_ref[cell]
            grads = geom_pull(geom, extra, d_rb, d_y)
            eg_ref[pl.ds(cell, 1), :] = jnp.concatenate(grads, 1)
            slot = stencil_of(nbr_ref[pl.ds(cell, 1), :])[3]
            pick = iota((slots, lanes), 0) == slot
            zero = jnp.zeros((slots, lanes), F32)
            x_hi, x_lo = split32(jnp.concatenate([jnp.where(pick, g, 0.0) for g in grads] + [zero], 0))
            hot = hotx_ref[cell]
            hots += [hot, hot]
            xs += [x_hi.astype(BF16), x_lo.astype(BF16)]
        sent[...] += mm(jnp.concatenate(hots, 1), jnp.concatenate(xs, 1), NT)

    loop(back0)
    sent5[...] = jnp.zeros_like(sent5)
    width = sent.shape[1]
    for r, at in enumerate(grid):
        sent5[at + (slice(None), slice(0, width))] = sent[r : r + 1, :]
    copies = exchange(sent5, srecv, ext_face, ext_face, send_sem, recv_sem, 3 * n_o)
    force_ref[...] = lax.dot_general(
        eg_ref[...], expand_mat(slots, lanes), (NT, ((), ())),
        precision=lax.Precision.HIGHEST, preferred_element_type=F32,
    )
    fold5[...] = sent5[inner]
    for o, copy in zip(OFFSETS, copies):
        copy.wait()
        at = face(opposite(o), dims)
        fold5[at] = fold5[at] + srecv[halo(o, dims)]
    for r, at in enumerate(itertools.product(*[range(d) for d in dims])):
        force_ref[r : r + 1, :] = force_ref[r : r + 1, :] - fold5[at]


def shards(positions, species, neighbors, edge_mask, species_embed, radial_weight, mix_weight, readout, energy_offset):
    X, Y, Z, slots, edges = neighbors.shape
    dims = (X, Y, Z)
    cells = X * Y * Z
    atoms = cells * slots
    lanes = slots * edges
    ns, c = species_embed.shape
    nb = radial_weight.shape[1]
    ext = (X + 2, Y + 2, Z + 2)
    rows = ext[0] * ext[1] * ext[2]
    near = -(-27 * slots // 256) * 256

    nbr = jnp.where(edge_mask != 0, neighbors, NO_EDGE).reshape(cells, lanes)
    four = jnp.concatenate([positions, species[..., None].astype(F32)], -1)
    own_tab = jnp.swapaxes(four, -1, -2).reshape(cells, 4 * slots)
    own_tab = jnp.pad(own_tab, ((0, 0), (0, lanes - 4 * slots)))
    vm = pltpu.VMEM
    count = 4 * len(OFFSETS)
    smem = pl.BlockSpec(memory_space=pltpu.SMEM)
    energy, forces = pl.pallas_call(
        functools.partial(kernel, dims, slots, edges, nb),
        out_shape=[jax.ShapeDtypeStruct((1, atoms), F32), jax.ShapeDtypeStruct((cells, lanes), F32)],
        in_specs=[VM] * 8 + [smem],
        out_specs=[VM, VM],
        scratch_shapes=[
            vm(ext + (1, lanes), F32),
            vm((rows, lanes), F32),
            vm((cells, 3 * lanes), F32),
            vm((cells, near, lanes), BF16),
            vm((cells, rows, lanes), BF16),
            vm((cells, 8, lanes), F32),
            vm((cells, 18 * slots, lanes), BF16),
            vm((ns * nb, 3 * c), F32),
            vm((9, atoms, ns * nb), F32),
            vm((2, 9, atoms, c), F32),
            vm((9, atoms, c), F32),
            vm((atoms, c), F32),
            vm(dims + (slots, c), F32),
            vm(ext + (slots, c), F32),
            vm((cells * lanes, 3 * c), F32),
            vm((cells * lanes, c), F32),
            vm((cells, 3, 2 * lanes, c), BF16),
            vm((cells, 2 * lanes, 3 * c), BF16),
            vm(ext + (slots, c), F32),
            vm(ext + (slots, c), F32),
            vm((cells, nb, lanes), F32),
            vm((cells, 16, lanes), F32),
            vm(dims + (slots, c), F32),
            vm((cells, 3 * lanes), F32),
            vm((rows, 4 * slots), F32),
            vm(ext + (1, lanes), F32),
            vm(ext + (1, lanes), F32),
            vm(dims + (1, lanes), F32),
            pltpu.SemaphoreType.DMA((count,)),
            pltpu.SemaphoreType.DMA((count,)),
            pltpu.SemaphoreType.DMA((2,)),
        ],
        compiler_params=pltpu.CompilerParams(
            collective_id=1, has_side_effects=True, vmem_limit_bytes=58 * 1024 * 1024
        ),
        name="potential",
    )(
        own_tab.reshape(X, Y, Z, 1, lanes), own_tab, nbr, species.reshape(1, atoms), species_embed,
        radial_weight, mix_weight, readout.reshape(1, c), energy_offset.reshape(1, ns),
    )
    forces = forces[:, : 3 * slots].reshape(X, Y, Z, 3, slots)
    return energy.reshape(X, Y, Z, slots), jnp.swapaxes(forces, -1, -2)


def solution(mesh):
    g = P("gx", "gy", "gz")
    return jax.shard_map(
        shards,
        mesh=mesh,
        in_specs=(g, g, g, g, P(), P(), P(), P(), P()),
        out_specs=(g, g),
        check_vma=False,
    )
```

time: 132 us -> 69.8 us (0.53)
  Pallas kernels: 116 us -> 61.3 us
  other arithmetic: 6.01 us -> 2.26 us
  local copies, waits for them, and re-layouts: 8.06 us -> 5.04 us
    pallas_call x7 -> x1, Pallas kernels: 116 us -> 61.3 us  [shards(): pl.pallas_call(functools.partial(kernel, dims, slots, edges, nb), out_sha...]
    select_n x2 -> x0, other arithmetic: 4.14 us -> none  [the longest x1 3.29 us: shards(): offset = jnp.where(flat_species == s, energy_offset[s], offset)]
    squeeze x3 -> x0, local copies, waits for them, and re-layouts: 3.25 us -> none  [the longest x1 1.8 us: shards(): mix_weight[1]]
    slice x1 -> x0, local copies, waits for them, and re-layouts: 1.44 us -> none  [shards(): offset = jnp.where(flat_species == s, energy_offset[s], offset)]
    reshape x1 -> x2, local copies, waits for them, and re-layouts: 0.09 us -> 1.44 us  [the longest x1 0.8 us: shards(): forces = forces[:, :3 * slots].reshape(X, Y, Z, 3, slots)]
where the time goes in v1:
time: 69.8 us; the launch traced here: 69.3 us
  Pallas kernels  61.3 us (88%)
  local copies, waits for them, and re-layouts  5.04 us (7%)
  other arithmetic  2.26 us (3%)
    pallas_call x1, Pallas kernels, shards(): pl.pallas_call(functools.partial(kernel, dims, slots, edges, nb), out_sha...  61.3 us

profile of v1, /device:TPU:0, one launch (start us, length us, event | category | flops | bytes accessed | tf_op | source)
XLA Modules:
  0.0 69.3 jit_solution(13922639201778053757)
XLA Ops:
  0.6 0.7 %convert_bitcast_fusion = f32[2,4,4,8,1]{3,2,4,1,0:T(4,128)S(1)} fusion(s32[2,4,4,8]{3,2,1,0:T(4,128)} %param.10), kind=kLoop, calls=%fused_computation.2 | loop fusion | flops 256 | bytes 2048 | tf_op jit(solution)/shard_map/convert_element_type | solution.py:553
  1.4 0.0 copy-start.1
  1.4 0.9 %maximum_bitcast_fusion = f32[2,4,4,4,8]{4,2,3,1,0:T(4,128)S(1)} fusion(f32[2,4,4,8,1]{3,2,4,1,0:T(4,128)S(1)} %convert_bitcast_fusion, f32[2,4,4,8,3]{3,2,4,1,0:T(4,128)} %param.9), kind=kLoop, calls=%fused_computation.1 | loop fusion | flops 1024 | bytes 8192 | tf_op jit(solution)/shard_map/transpose | solution.py:554
  2.2 0.0 copy-start
  2.2 0.1 reshape.29
  2.3 0.6 pad.4.own_ref
  3.0 0.0 copy-done.1
  3.0 0.2 copy-done
  3.2 0.0 copy-start.2
  3.2 0.7 %reshape.31.nbr_ref = s32[32,128]{1,0:T(8,128)} reshape(s32[2,4,4,8,16]{4,3,2,1,0:T(8,128)S(1)} %compare_select_fusion) | data formatting | bytes 32768 | tf_op jit(solution)/shard_map/reshape | solution.py:552
  3.9 0.0 copy-done.2
  3.9 0.6 reshape.32.spec_ref
  4.5 61.3 %potential.1 = (f32[1,256]{1,0:T(1,128)}, f32[32,128]{1,0:T(8,128)}) custom-call(f32[2,4,4,1,128]{4,3,2,1,0:T(1,128)} %bitcast.16, f32[32,128]{1,0:T(8,128)} %pad.4.own_ref, s32[32,128]{1,0:T(8,128)} %reshape.31.nbr_ref, s32[1,256]{1,0:T(1,128)} %reshape.32.spec_ref, f32[4,128]{1,0:T(4,128)} %emb_ref.1, f32[2,8,384]{2,1,0:T(8,128)} %w_ref.1, ...), custom_call_target="tpu_custom_call" | custom-call | tf_op jit(solution)/shard_map/potential/pallas_call | solution.py:559
  65.8 0.8 %reshape.36 = f32[2,4,4,3,8]{4,3,2,1,0:T(4,128)S(1)} reshape(f32[32,24]{1,0:T(8,128)} %bitcast.17) | data formatting | bytes 6144 | tf_op jit(solution)/shard_map/reshape | solution.py:605
  66.6 0.6 copy.18
  67.3 0.0 copy-start.3
  67.3 0.5 broadcast.5
  67.8 0.1 copy-done.3
  67.9 0.7 reduce.3
  68.6 0.7 %reshape.35 = f32[2,4,4,8]{3,2,1,0:T(4,128)} reshape(f32[256]{0:T(256)S(1)} %reduce.3) | data formatting | bytes 2048 | tf_op jit(solution)/shard_map/reshape | solution.py:606
  (2 shorter events, 0.0 us)
Async XLA Ops:
  1.4 1.6 %copy-start.1 = (s32[2,4,4,8,16]{4,3,2,1,0:T(8,128)S(1)}, s32[2,4,4,8,16]{4,3,2,1,0:T(8,128)}, u32[]{:S(2)}) copy-start(s32[2,4,4,8,16]{4,3,2,1,0:T(8,128)} %param.12) | copy-start | bytes 49156
  2.2 0.9 %copy-start = (s32[2,4,4,8,16]{4,3,2,1,0:T(8,128)S(1)}, s32[2,4,4,8,16]{4,3,2,1,0:T(8,128)}, u32[]{:S(2)}) copy-start(s32[2,4,4,8,16]{4,3,2,1,0:T(8,128)} %param.11) | copy-start | bytes 49156
  3.2 0.7 %copy-start.2 = (s32[2,4,4,8]{3,2,1,0:T(4,128)S(1)}, s32[2,4,4,8]{3,2,1,0:T(4,128)}, u32[]{:S(2)}) copy-start(s32[2,4,4,8]{3,2,1,0:T(4,128)} %param.10) | copy-start | bytes 3076
  67.3 0.6 copy-start.3

commit v2 on v1

--- a/solution.py
+++ b/solution.py
@@ -14,7 +14,7 @@
 MESH = pl.DeviceIdType.MESH
 AXES = ("gx", "gy", "gz")
 RC = 2.0
-NO_EDGE = 1023
+NO_EDGE = 256
 OFFSETS = [o for o in itertools.product((-1, 0, 1), repeat=3) if any(o)]
 ORDERS = ((0, 1), (1, 4), (4, 9))
 VM = pl.BlockSpec(memory_space=pltpu.VMEM)
@@ -219,8 +219,9 @@
     return copies
 
 
-def kernel(dims, slots, edges, nb, own5_ref, own_ref, nbr_ref, spec_ref, emb_ref, w_ref, mix_ref, read_ref,
-           off_ref, energy_ref, force_ref,
+def kernel(dims, slots, edges, nb, pos_ref, sp_ref, nb_ref, em_ref, emb_ref, w_ref, mix_ref, read_ref,
+           off_ref, energy_ref, out_ref,
+           own5_ref, own_ref, nbr_ref, spec_ref, force_ref,
            tab_ext, tab2, own_pos, hot_ref, hotx_ref, geom_ref, ym_ref, we_ref, v_ref, a_ref, g_ref,
            dsilu_ref, hid_own, hid_ext, rad_ref, h_ref, t_ref, z_ref, dext, drecv, drb_ref, dy_ref,
            dh_ref, eg_ref, sent, sent5, srecv, fold5, send_sem, recv_sem, local_sem):
@@ -270,6 +271,22 @@
             hot_ref[cell] = hot_rows(n, near_pad)
             hotx_ref[cell] = ext_hot(n, rows, base_of(cx, cy, cz), ye, ze)[0].astype(BF16)
 
+    own_ref[...] = jnp.zeros_like(own_ref)
+    for i in range(X * Y):
+        cx, cy = i // Y, i % Y
+        block = pl.ds(i * Z, Z)
+        for k in range(3):
+            own_ref[block, k * slots : (k + 1) * slots] = pos_ref[cx, cy, k]
+        own_ref[block, 3 * slots : 4 * slots] = sp_ref[cx, cy].astype(F32)
+        for cz in range(Z):
+            cell = i * Z + cz
+            spec_ref[0:1, cell * slots : (cell + 1) * slots] = sp_ref[cx, cy, cz : cz + 1, :]
+            own5_ref[cx, cy, cz] = own_ref[cell : cell + 1, :]
+    coded = jnp.where(em_ref[...] != 0, nb_ref[...], NO_EDGE).reshape(atoms, edges).astype(F32)
+    lane = iota((edges, lanes), 1)
+    repeat = jnp.where((lane & (edges - 1)) == iota((edges, lanes), 0), 1.0, 0.0).astype(BF16)
+    wide = mm(coded.astype(BF16), repeat, NN).reshape(cells, slots, lanes)
+    nbr_ref[...] = jnp.sum(wide * mask[None], 1).astype(jnp.int32)
     loop(build_hot)
     pl.semaphore_wait(barrier, n_o)
 
@@ -440,8 +457,9 @@
     read8 = jnp.concatenate([read] * 8, 0)
     energy = mm3(split(read8), split(hid2), NT)[0:1]
     for k in range(ns):
-        energy = energy + jnp.where(spec_row == k, off_ref[0, k], 0.0)
-    energy_ref[...] = energy
+        energy = energy + jnp.where(spec_row == k, off_ref[k], 0.0)
+    for r, (cx, cy, cz) in enumerate(itertools.product(*[range(d) for d in dims])):
+        energy_ref[cx, cy, cz : cz + 1, :] = energy[:, r * slots : (r + 1) * slots]
     w_rows = rows_hl(w1)
 
     def pull_rows(full, first, count):
@@ -535,6 +553,9 @@
         fold5[at] = fold5[at] + srecv[halo(o, dims)]
     for r, at in enumerate(itertools.product(*[range(d) for d in dims])):
         force_ref[r : r + 1, :] = force_ref[r : r + 1, :] - fold5[at]
+    for i in range(X * Y):
+        for k in range(3):
+            out_ref[i // Y, i % Y, k] = force_ref[pl.ds(i * Z, Z), k * slots : (k + 1) * slots]
 
 
 def shards(positions, species, neighbors, edge_mask, species_embed, radial_weight, mix_weight, readout, energy_offset):
@@ -549,19 +570,23 @@
     rows = ext[0] * ext[1] * ext[2]
     near = -(-27 * slots // 256) * 256
 
-    nbr = jnp.where(edge_mask != 0, neighbors, NO_EDGE).reshape(cells, lanes)
-    four = jnp.concatenate([positions, species[..., None].astype(F32)], -1)
-    own_tab = jnp.swapaxes(four, -1, -2).reshape(cells, 4 * slots)
-    own_tab = jnp.pad(own_tab, ((0, 0), (0, lanes - 4 * slots)))
     vm = pltpu.VMEM
     count = 4 * len(OFFSETS)
     smem = pl.BlockSpec(memory_space=pltpu.SMEM)
     energy, forces = pl.pallas_call(
         functools.partial(kernel, dims, slots, edges, nb),
-        out_shape=[jax.ShapeDtypeStruct((1, atoms), F32), jax.ShapeDtypeStruct((cells, lanes), F32)],
+        out_shape=[
+            jax.ShapeDtypeStruct(dims + (slots,), F32),
+            jax.ShapeDtypeStruct((X, Y, 3, Z, slots), F32),
+        ],
         in_specs=[VM] * 8 + [smem],
         out_specs=[VM, VM],
         scratch_shapes=[
+            vm(dims + (1, lanes), F32),
+            vm((cells, lanes), F32),
+            vm((cells, lanes), jnp.int32),
+            vm((1, atoms), jnp.int32),
+            vm((cells, lanes), F32),
             vm(ext + (1, lanes), F32),
             vm((rows, lanes), F32),
             vm((cells, 3 * lanes), F32),
@@ -599,11 +624,10 @@
         ),
         name="potential",
     )(
-        own_tab.reshape(X, Y, Z, 1, lanes), own_tab, nbr, species.reshape(1, atoms), species_embed,
-        radial_weight, mix_weight, readout.reshape(1, c), energy_offset.reshape(1, ns),
+        jnp.transpose(positions, (0, 1, 4, 2, 3)), species, neighbors, edge_mask, species_embed,
+        radial_weight, mix_weight, readout.reshape(1, c), energy_offset,
     )
-    forces = forces[:, : 3 * slots].reshape(X, Y, Z, 3, slots)
-    return energy.reshape(X, Y, Z, slots), jnp.swapaxes(forces, -1, -2)
+    return energy, jnp.transpose(forces, (0, 1, 3, 4, 2))
 
 
 def solution(mesh):

time: 69.8 us -> 65.2 us (0.934)
  local copies, waits for them, and re-layouts: 5.04 us -> 2.75 us
  other arithmetic: 2.26 us -> 0 us
    reshape x5 -> x0, local copies, waits for them, and re-layouts: 2.95 us -> none  [the longest x1 0.8 us: shards(): forces = forces[:, :3 * slots].reshape(X, Y, Z, 3, slots)]
    unnamed x9 -> x2, local copies, waits for them, and re-layouts: 0.95 us -> 2.75 us
    transpose x1 -> x0, other arithmetic: 0.85 us -> none  [shards(): own_tab = jnp.swapaxes(four, -1, -2).reshape(cells, 4 * slots)]
    convert_element_type x1 -> x0, other arithmetic: 0.72 us -> none  [shards(): four = jnp.concatenate([positions, species[..., None].astype(F32)], -1)]
where the time goes in v2:
time: 65.2 us; the launch traced here: 64.9 us
  Pallas kernels  61.5 us (94%)
  local copies, waits for them, and re-layouts  2.75 us (4%)
    pallas_call x1, Pallas kernels, shards(): pl.pallas_call(functools.partial(kernel, dims, slots, edges, nb), out_sha...  61.5 us
    unnamed x2, local copies, waits for them, and re-layouts  2.75 us

profile of v2, /device:TPU:0, one launch (start us, length us, event | category | flops | bytes accessed | tf_op | source)
XLA Modules:
  0.0 64.9 jit_solution(15724181338950221012)
XLA Ops:
  0.6 61.5 %potential.1 = (f32[2,4,4,8]{3,2,1,0:T(4,128)}, f32[2,4,3,4,8]{4,3,2,1,0:T(4,128)}) custom-call(f32[2,4,3,4,8]{4,3,2,1,0:T(4,128)} %bitcast.3, s32[2,4,4,8]{3,2,1,0:T(4,128)} %sp_ref.1, s32[2,4,4,8,16]{4,3,2,1,0:T(8,128)} %nb_ref.1, s32[2,4,4,8,16]{4,3,2,1,0:T(8,128)} %em_ref.1, f32[4,128]{1,0:T(4,128)} %emb_ref.1, f32[2,8,384]{2,1,0:T(8,128)} %w_ref.1, ...), custom_call_target="tpu_custom_call" | custom-call | tf_op jit(solution)/shard_map/potential/pallas_call | solution.py:576
  62.2 1.3 %copy.13 = f32[2,4,4,8]{3,2,1,0:T(4,128)} copy(f32[2,4,4,8]{3,2,1,0:T(4,128)} %get-tuple-element.8) | data formatting | bytes 2048
  63.5 1.4 %copy.14 = f32[2,4,4,8,3]{3,2,4,1,0:T(4,128)} copy(f32[2,4,4,8,3]{3,2,4,1,0:T(4,128)} %bitcast.4) | data formatting | bytes 6144

commit v3 on v2

--- a/solution.py
+++ b/solution.py
@@ -15,7 +15,7 @@
 AXES = ("gx", "gy", "gz")
 RC = 2.0
 NO_EDGE = 256
-OFFSETS = [o for o in itertools.product((-1, 0, 1), repeat=3) if any(o)]
+OFFSETS = sorted((o for o in itertools.product((-1, 0, 1), repeat=3) if any(o)), key=lambda o: -o[0])
 ORDERS = ((0, 1), (1, 4), (4, 9))
 VM = pl.BlockSpec(memory_space=pltpu.VMEM)
 
@@ -202,9 +202,11 @@
     return jnp.concatenate([ys[m] * mask for m in range(lo, hi)], 0)
 
 
-def exchange(src, dst, src_at, dst_at, send_sem, recv_sem, base):
+def exchange(src, dst, src_at, dst_at, send_sem, recv_sem, base, only=(-1, 0, 1)):
     copies = []
     for i, o in enumerate(OFFSETS):
+        if o[0] not in only:
+            continue
         copies.append(
             pltpu.make_async_remote_copy(
                 src_ref=src.at[src_at(o)],
@@ -220,7 +222,7 @@
 
 
 def kernel(dims, slots, edges, nb, pos_ref, sp_ref, nb_ref, em_ref, emb_ref, w_ref, mix_ref, read_ref,
-           off_ref, energy_ref, out_ref,
+           off_ref, out_ref,
            own5_ref, own_ref, nbr_ref, spec_ref, force_ref,
            tab_ext, tab2, own_pos, hot_ref, hotx_ref, geom_ref, ym_ref, we_ref, v_ref, a_ref, g_ref,
            dsilu_ref, hid_own, hid_ext, rad_ref, h_ref, t_ref, z_ref, dext, drecv, drb_ref, dy_ref,
@@ -251,12 +253,12 @@
     def base_of(cx, cy, cz):
         return ((cx + 1) * ye + cy + 1) * ze + cz + 1
 
-    def loop(body):
+    def loop(body, first=0, last=X * Y):
         def step(i, carry):
             cx, cy = i // Y, i % Y
             body(i, cx, cy)
             return carry
-        lax.fori_loop(0, X * Y, step, 0)
+        lax.fori_loop(first, last, step, 0)
 
     def edge_rows(cell):
         return pl.ds(pl.multiple_of(cell * lanes, lanes), lanes)
@@ -382,7 +384,8 @@
 
     loop(radials)
     local.wait()
-    for copy in copies:
+    late = sum(o[0] == -1 for o in OFFSETS)
+    for copy in copies[:-late]:
         copy.wait()
 
     def layer1(i, cx, cy):
@@ -415,7 +418,10 @@
                 for m in range(lo, hi):
                     a_ref[1, m, atom_rows(cell), :] = sums[(m - lo) * slots : (m - lo + 1) * slots]
 
-    loop(layer1)
+    loop(layer1, 0, (X - 1) * Y)
+    for copy in copies[-late:]:
+        copy.wait()
+    loop(layer1, (X - 1) * Y)
     read = read_ref[...]
     v = mm3(split(invariants_of(a_ref.at[1])), split(mix_ref[1]), NN)
     up, slope = silu_parts(v)
@@ -450,8 +456,10 @@
                 part = sums[j * 3 * slots : (j + 1) * 3 * slots].reshape(3, slots, c)
                 dext[at] = dext[at] + part
 
-    loop(back1)
-    copies = exchange(dext, drecv, ext_face, ext_face, send_sem, recv_sem, 2 * n_o)
+    loop(back1, 0, Y)
+    early = exchange(dext, drecv, ext_face, ext_face, send_sem, recv_sem, 2 * n_o, (-1,))
+    loop(back1, Y)
+    copies = exchange(dext, drecv, ext_face, ext_face, send_sem, recv_sem, 2 * n_o, (0, 1)) + early
 
     hid2 = hid_ext[1 : X + 1, 1 : Y + 1, 1 : Z + 1].reshape(atoms, c) + up
     read8 = jnp.concatenate([read] * 8, 0)
@@ -459,7 +467,7 @@
     for k in range(ns):
         energy = energy + jnp.where(spec_row == k, off_ref[k], 0.0)
     for r, (cx, cy, cz) in enumerate(itertools.product(*[range(d) for d in dims])):
-        energy_ref[cx, cy, cz : cz + 1, :] = energy[:, r * slots : (r + 1) * slots]
+        out_ref[cx, cy, 3, cz : cz + 1, :] = energy[:, r * slots : (r + 1) * slots]
     w_rows = rows_hl(w1)
 
     def pull_rows(full, first, count):
@@ -573,14 +581,11 @@
     vm = pltpu.VMEM
     count = 4 * len(OFFSETS)
     smem = pl.BlockSpec(memory_space=pltpu.SMEM)
-    energy, forces = pl.pallas_call(
+    both = pl.pallas_call(
         functools.partial(kernel, dims, slots, edges, nb),
-        out_shape=[
-            jax.ShapeDtypeStruct(dims + (slots,), F32),
-            jax.ShapeDtypeStruct((X, Y, 3, Z, slots), F32),
-        ],
+        out_shape=jax.ShapeDtypeStruct((X, Y, 4, Z, slots), F32),
         in_specs=[VM] * 8 + [smem],
-        out_specs=[VM, VM],
+        out_specs=VM,
         scratch_shapes=[
             vm(dims + (1, lanes), F32),
             vm((cells, lanes), F32),
@@ -627,7 +632,7 @@
         jnp.transpose(positions, (0, 1, 4, 2, 3)), species, neighbors, edge_mask, species_embed,
         radial_weight, mix_weight, readout.reshape(1, c), energy_offset,
     )
-    return energy, jnp.transpose(forces, (0, 1, 3, 4, 2))
+    return both[:, :, 3], jnp.transpose(both[:, :, :3], (0, 1, 3, 4, 2))
 
 
 def solution(mesh):

time: 65.2 us -> 62.1 us (0.952)
  Pallas kernels: 61.5 us -> 58.5 us
    pallas_call x1, Pallas kernels: 61.5 us -> 58.5 us  [shards(): pl.pallas_call(functools.partial(kernel, dims, slots, edges, nb), out_sha...]
    unnamed x2 -> x0, local copies, waits for them, and re-layouts: 2.75 us -> none
    transpose x0 -> x1, local copies, waits for them, and re-layouts: none -> 1.42 us  [shards(): return (both[:, :, 3], jnp.transpose(both[:, :, :3], (0, 1, 3, 4, 2)))]
    squeeze x0 -> x1, local copies, waits for them, and re-layouts: none -> 1.32 us  [shards(): return (both[:, :, 3], jnp.transpose(both[:, :, :3], (0, 1, 3, 4, 2)))]
where the time goes in v3:
time: 62.1 us; the launch traced here: 61.9 us
  Pallas kernels  58.5 us (94%)
  local copies, waits for them, and re-layouts  2.75 us (4%)
  between operations  0.64 us (1%)
    pallas_call x1, Pallas kernels, shards(): pl.pallas_call(functools.partial(kernel, dims, slots, edges, nb), out_sha...  58.5 us
    transpose x1, local copies, waits for them, and re-layouts, shards(): return (both[:, :, 3], jnp.transpose(both[:, :, :3], (0, 1, 3, 4, 2)))  1.42 us
    squeeze x1, local copies, waits for them, and re-layouts, shards(): return (both[:, :, 3], jnp.transpose(both[:, :, :3], (0, 1, 3, 4, 2)))  1.32 us

profile of v3, /device:TPU:0, one launch (start us, length us, event | category | flops | bytes accessed | tf_op | source)
XLA Modules:
  0.0 61.9 jit_solution(13478967070823600677)
XLA Ops:
  0.6 58.5 %potential.1 = f32[2,4,4,4,8]{4,3,2,1,0:T(4,128)} custom-call(f32[2,4,3,4,8]{4,3,2,1,0:T(4,128)} %bitcast.6, s32[2,4,4,8]{3,2,1,0:T(4,128)} %sp_ref.1, s32[2,4,4,8,16]{4,3,2,1,0:T(8,128)} %nb_ref.1, s32[2,4,4,8,16]{4,3,2,1,0:T(8,128)} %em_ref.1, f32[4,128]{1,0:T(4,128)} %emb_ref.1, f32[2,8,384]{2,1,0:T(8,128)} %w_ref.1, f32[2,384,128]{2,1,0:T(8,128)} %mix_ref.1, ...), custom_call_target="tpu_custom_call" | custom-call | tf_op jit(solution)/shard_map/potential/pallas_call | solution.py:584
  59.1 1.3 %slice_bitcast_fusion.1 = f32[2,4,4,8]{3,2,1,0:T(4,128)} fusion(f32[2,4,4,4,8]{4,3,2,1,0:T(4,128)} %potential.1), kind=kLoop, calls=%fused_computation.1 | loop fusion | bytes 2048 | tf_op jit(solution)/shard_map/squeeze | solution.py:635
  60.5 1.4 %slice_bitcast_fusion = f32[2,4,4,8,3]{3,2,4,1,0:T(4,128)} fusion(f32[2,4,4,4,8]{4,3,2,1,0:T(4,128)} %potential.1), kind=kLoop, calls=%fused_computation | loop fusion | bytes 6144 | tf_op jit(solution)/shard_map/transpose | solution.py:635
